TPU v7x, 32 devices: a whole 2x2x4 slice. The times are simulated.
32 devices in a mesh: data: 8 (over z, y), width: 4 (over x, core).
Axes of the slice: x: 2, y: 2, z: 4, core: 2. Of those that a mesh axis runs over, the one named last changes fastest.
Arguments:
- grad_up: float32 [8, 768, 3072], P('data', None, 'width'), may hold values from -4 to 4
- grad_down: float32 [8, 3072, 768], P('data', 'width'), may hold values from -4 to 4
- grad_query: float32 [8, 768, 768], P('data', None, 'width'), may hold values from -4 to 4
- grad_key: float32 [8, 768, 768], P('data', None, 'width'), may hold values from -4 to 4
- grad_value: float32 [8, 768, 768], P('data', None, 'width'), may hold values from -4 to 4
- grad_mixed: float32 [8, 768, 768], P('data', 'width'), may hold values from -4 to 4
- grad_norm: float32 [8, 768], P('data'), may hold values from -8 to 8
- weight_up: float32 [768, 3072], P('data', 'width'), may hold values from -0.21875 to 0.21875
- weight_down: float32 [3072, 768], P('width', 'data'), may hold values from -0.109375 to 0.109375
- weight_query: float32 [768, 768], P('data', 'width'), may hold values from -0.21875 to 0.21875
- weight_key: float32 [768, 768], P('data', 'width'), may hold values from -0.21875 to 0.21875
- weight_value: float32 [768, 768], P('data', 'width'), may hold values from -0.21875 to 0.21875
- weight_mixed: float32 [768, 768], P('width', 'data'), may hold values from -0.21875 to 0.21875
- weight_norm: float32 [768], P('data'), may hold values from 0.25 to 1.75
- moment_up: float32 [768, 3072], P('data', 'width'), may hold values from 0.05 to 0.8
- moment_down: float32 [3072, 768], P('width', 'data'), may hold values from 0.05 to 0.8
- moment_query: float32 [768, 768], P('data', 'width'), may hold values from 0.05 to 0.8
- moment_key: float32 [768, 768], P('data', 'width'), may hold values from 0.05 to 0.8
- moment_value: float32 [768, 768], P('data', 'width'), may hold values from 0.05 to 0.8
- moment_mixed: float32 [768, 768], P('width', 'data'), may hold values from 0.05 to 0.8
- moment_norm: float32 [768], P('data'), may hold values from 0.05 to 0.8
Outputs:
- copy_up: bfloat16 [768, 3072], P(None, 'width')
- copy_down: bfloat16 [3072, 768], P('width')
- copy_query: bfloat16 [768, 768], P(None, 'width')
- copy_key: bfloat16 [768, 768], P(None, 'width')
- copy_value: bfloat16 [768, 768], P(None, 'width')
- copy_mixed: bfloat16 [768, 768], P('width')
- copy_norm: bfloat16 [768], replicated
- new_up: float32 [768, 3072], P('data', 'width')
- new_down: float32 [3072, 768], P('width', 'data')
- new_query: float32 [768, 768], P('data', 'width')
- new_key: float32 [768, 768], P('data', 'width')
- new_value: float32 [768, 768], P('data', 'width')
- new_mixed: float32 [768, 768], P('width', 'data')
- new_norm: float32 [768], P('data')
- state_new_up: float32 [768, 3072], P('data', 'width')
- state_new_down: float32 [3072, 768], P('width', 'data')
- state_new_query: float32 [768, 768], P('data', 'width')
- state_new_key: float32 [768, 768], P('data', 'width')
- state_new_value: float32 [768, 768], P('data', 'width')
- state_new_mixed: float32 [768, 768], P('width', 'data')
- state_new_norm: float32 [768], P('data')
All inputs are finite; a program needn't handle non-finite values.
Results may differ from a plain program's by a relative error of at most 0.0004.
Values may be sent and summed in bfloat16 or wider, within the bound.
A program may use at most 128 MiB of HBM per device.

v0:
```python
import functools

import jax
import jax.numpy as jnp
from jax import lax
from jax.experimental import pallas as pl
from jax.experimental.pallas import tpu as pltpu
from jax.sharding import PartitionSpec as P

learn_rate = 0.05
hold_rate = 0.9
LANES = 128
SUB = 8


def round_up(value, unit):
    return -(-value // unit) * unit


def turn(block):
    rows, cols = block.shape
    tall, wide = round_up(rows, LANES), round_up(cols, LANES)
    if wide != cols:
        block = jnp.concatenate([block, jnp.zeros((rows, wide - cols), block.dtype)], axis=1)
    if tall != rows:
        block = jnp.concatenate([block, jnp.zeros((tall - rows, wide), block.dtype)], axis=0)
    return block.T[:cols, :rows]


def kernel(n, bits, rows, orders, *refs):
    refs = list(refs)
    take = lambda count: [refs.pop(0) for _ in range(count)]
    g_up, g_down, g_query, g_key, g_value, g_mixed, g_norm = take(7)
    w_up, w_down, w_query, w_key, w_value, w_mixed, w_norm = take(7)
    m_up, m_down, m_query, m_key, m_value, m_mixed, m_norm = take(7)
    c_up, c_down, c_query, c_key, c_value, c_mixed, c_norm = take(7)
    n_up, n_down, n_query, n_key, n_value, n_mixed, n_norm = take(7)
    s_up, s_down, s_query, s_key, s_value, s_mixed, s_norm = take(7)
    count = len(orders)
    part = take(count)
    held = [take(bits) for _ in range(count)]
    copies = take(count)
    send_sem, recv_sem = take(2)

    me = lax.axis_index("data")
    bit = [(me // 2**k) % 2 for k in range(bits)]
    partner = [me + 2**k * (1 - 2 * bit[k]) for k in range(bits)]

    barrier = pltpu.get_barrier_semaphore()
    for k in range(bits):
        pl.semaphore_signal(
            barrier, inc=1, device_id={"data": partner[k]}, device_id_type=pl.DeviceIdType.MESH
        )
    pl.semaphore_wait(barrier, bits)

    mean_rate = n ** (-0.5)
    half = g_up.shape[1] // 2
    heads = g_query.shape[0]
    mine = tuple(bit[k] for k in reversed(range(bits)))
    every = (slice(None),) * bits

    def index(chunk, step, own):
        fixed = {k: bit[k] for k in orders[chunk][:step]}
        if step < bits:
            k = orders[chunk][step]
            fixed[k] = bit[k] if own else 1 - bit[k]
        return tuple(fixed.get(k, slice(None)) for k in reversed(range(bits)))

    def copy(src, dst, chunk, slot, k):
        return pltpu.make_async_remote_copy(
            src_ref=src,
            dst_ref=dst,
            send_sem=send_sem.at[chunk, slot],
            recv_sem=recv_sem.at[chunk, slot],
            device_id={"data": partner[k]},
            device_id_type=pl.DeviceIdType.MESH,
        )

    def scatter(chunk, step):
        return copy(
            part[chunk].at[index(chunk, step, False)],
            held[chunk][step],
            chunk,
            step,
            orders[chunk][step],
        )

    def gather(chunk, step):
        there = copies[chunk].at[index(chunk, step, True)]
        return copy(there, there, chunk, bits + step, orders[chunk][step])

    def tile_loop(body):
        def step(i, carry):
            body(pl.multiple_of(i * SUB, SUB))
            return carry

        lax.fori_loop(0, rows // SUB, step, 0)

    def blocks(value):
        return value.reshape((2,) * bits + (rows, value.shape[-1]))

    def fill_up(h):
        def fill(chunk):
            for d in range(n):
                where = tuple((d >> k) & 1 for k in reversed(range(bits)))

                def body(r):
                    part[chunk][where + (pl.ds(r, SUB), slice(None))] = g_up[
                        pl.ds(pl.multiple_of(d * rows + r, SUB), SUB), h * half : (h + 1) * half
                    ]

                tile_loop(body)

        return fill

    def fill_down(h):
        def fill(chunk):
            for j in range(half // LANES):
                block = g_down[h * half + j * LANES : h * half + (j + 1) * LANES, :]
                part[chunk][every + (slice(None), slice(j * LANES, (j + 1) * LANES))] = blocks(turn(block))

        return fill

    def fill_pair(first, second):
        def fill(chunk):
            both = turn(jnp.concatenate([first[...], second[...]], axis=0))
            part[chunk][...] = blocks(both)

        return fill

    def fill_norm(chunk):
        for d in range(n):
            where = tuple((d >> k) & 1 for k in reversed(range(bits)))
            part[chunk][where] = jnp.zeros_like(part[chunk][where])
            part[chunk][where + (slice(0, 1), slice(0, rows))] = g_norm[d : d + 1, :]

    def update(total, weight, moment):
        mean = total * mean_rate
        state = hold_rate * moment + (1.0 - hold_rate) * mean * mean
        return weight - learn_rate * mean * lax.rsqrt(state + 1e-06), state

    def own(chunk, lanes):
        return part[chunk][mine + (slice(None), lanes)]

    def step_wide(h, weight, moment, n_out, s_out):
        def run(chunk):
            at = slice(h * half, (h + 1) * half)
            new, state = update(own(chunk, slice(None)), weight[:, at], moment[:, at])
            n_out[:, at] = new
            s_out[:, at] = state
            copies[chunk][mine] = new.astype(jnp.bfloat16)

        return run

    def step_query_key(chunk):
        weight = jnp.concatenate([w_query[...], w_key[...]], axis=1)
        moment = jnp.concatenate([m_query[...], m_key[...]], axis=1)
        new, state = update(own(chunk, slice(None)), weight, moment)
        copies[chunk][mine] = new.astype(jnp.bfloat16)
        n_query[...], n_key[...] = new[:, :heads], new[:, heads:]
        s_query[...], s_key[...] = state[:, :heads], state[:, heads:]

    def step_value_mixed(chunk):
        weight = jnp.concatenate([w_value[...], turn(w_mixed[...])], axis=1)
        moment = jnp.concatenate([m_value[...], turn(m_mixed[...])], axis=1)
        new, state = update(own(chunk, slice(None)), weight, moment)
        copies[chunk][mine] = new.astype(jnp.bfloat16)
        n_value[...], s_value[...] = new[:, :heads], state[:, :heads]
        n_mixed[...] = turn(new[:, heads:])
        s_mixed[...] = turn(state[:, heads:])

    def step_norm(chunk):
        new, state = update(part[chunk][mine][0:1, :rows], w_norm[...], m_norm[...])
        n_norm[...] = new
        s_norm[...] = state
        width = part[chunk].shape[-1]
        full = jnp.zeros((16, width), jnp.float32)
        if width != rows:
            new = jnp.concatenate([new, jnp.zeros((1, width - rows), jnp.float32)], axis=1)
        copies[chunk][mine] = (full + new).astype(jnp.bfloat16)

    group = 1 if rows % 16 == 0 else 2

    def end_rows(chunk, write):
        for d in range(0, n, group):
            got = [
                copies[chunk][tuple(((d + i) >> k) & 1 for k in reversed(range(bits)))] for i in range(group)
            ]
            if group > 1:
                got = [jnp.concatenate([g.astype(jnp.float32) for g in got], axis=0).astype(jnp.bfloat16)]
            write(slice(d * rows, (d + group) * rows), got[0])

    def end_up(h):
        def end(chunk):
            def write(at, value):
                c_up[at, h * half : (h + 1) * half] = value

            end_rows(chunk, write)

        return end

    def end_down(h):
        def end(chunk):
            for j in range(half // LANES):
                lanes = slice(j * LANES, (j + 1) * LANES)
                value = copies[chunk][every + (slice(None), lanes)].astype(jnp.float32)
                value = value.reshape(n * rows, LANES)
                c_down[h * half + j * LANES : h * half + (j + 1) * LANES, :] = turn(value).astype(jnp.bfloat16)

        return end

    def end_pair(first, second):
        def end(chunk):
            value = copies[chunk][...].astype(jnp.float32).reshape(n * rows, 2 * heads)
            both = turn(value)
            first[...] = both[:heads].astype(jnp.bfloat16)
            second[...] = both[heads:].astype(jnp.bfloat16)

        return end

    def end_norm(chunk):
        got = [
            copies[chunk][tuple((d >> k) & 1 for k in reversed(range(bits)))].astype(jnp.float32)[0:1, :rows]
            for d in range(n)
        ]
        for d in range(n):
            c_norm[d : d + 1, :] = got[d]

    plan = [
        (fill_up(0), step_wide(0, w_up, m_up, n_up, s_up), end_up(0)),
        (fill_up(1), step_wide(1, w_up, m_up, n_up, s_up), end_up(1)),
        (fill_norm, step_norm, end_norm),
        (fill_down(0), step_wide(0, w_down, m_down, n_down, s_down), end_down(0)),
        (fill_down(1), step_wide(1, w_down, m_down, n_down, s_down), end_down(1)),
        (fill_pair(g_value, g_mixed), step_value_mixed, end_pair(c_value, c_mixed)),
        (fill_pair(g_query, g_key), step_query_key, end_pair(c_query, c_key)),
    ]

    for chunk in range(count):
        plan[chunk][0](chunk)
        scatter(chunk, 0).start()

    def event(chunk, stage):
        if stage < bits:
            scatter(chunk, stage).wait()
            where = index(chunk, stage, True)

            def body(r):
                at = pl.ds(r, SUB)
                full = where + (at, slice(None))
                lead = (slice(None),) * (len(held[chunk][stage].shape) - 2)
                part[chunk][full] = part[chunk][full] + held[chunk][stage][lead + (at, slice(None))]

            def step(i, carry):
                body(pl.multiple_of(i * SUB, SUB))
                return carry

            lax.fori_loop(0, part[chunk].shape[-2] // SUB, step, 0)
            if stage + 1 < bits:
                scatter(chunk, stage + 1).start()
            else:
                plan[chunk][1](chunk)
                gather(chunk, bits - 1).start()
        else:
            step = 2 * bits - 1 - stage
            gather(chunk, step).wait()
            if step > 0:
                gather(chunk, step - 1).start()
            else:
                plan[chunk][2](chunk)

    ahead = []
    for chunk in range(count):
        for stage in range(2 * bits):
            late = 0.75 * stage if stage < 2 * bits - 1 else max(0.5 * stage, count + 0.5 - 0.5 * chunk)
            ahead.append((chunk + late, chunk, stage))
    for _, chunk, stage in sorted(ahead):
        event(chunk, stage)


def hand_on(count, *refs):
    given, out, held, sem = refs[:count], refs[count : 2 * count], refs[2 * count : 3 * count], refs[3 * count]
    reads = [pltpu.make_async_copy(given[i], held[i], sem.at[0, i]) for i in range(count)]
    writes = [pltpu.make_async_copy(held[i], out[i], sem.at[1, i]) for i in range(count)]
    for read in reads:
        read.start()
    for read, write in zip(reads, writes):
        read.wait()
        write.start()
    for write in writes:
        write.wait()


def solution(mesh):
    n = mesh.shape["data"]
    bits = n.bit_length() - 1

    def on_device(*args):
        grads, weights, moments = args[:7], args[7:14], args[14:]
        rows = weights[0].shape[0]
        grads = [g[0].T if i in (2, 3, 4) else g[0] for i, g in enumerate(grads[:6])] + [grads[6].reshape(n, rows)]
        weights = list(weights[:6]) + [weights[6].reshape(1, rows)]
        moments = list(moments[:6]) + [moments[6].reshape(1, rows)]
        weights[1], moments[1] = weights[1].T, moments[1].T
        half, heads = grads[0].shape[1] // 2, grads[2].shape[0]
        near = tuple(range(bits))
        wide = round_up(rows, LANES)
        sizes = [(rows, half)] * 2 + [(SUB, wide)] + [(rows, half)] * 2 + [(rows, 2 * heads)] * 2
        orders = [near] * 7
        copy_sizes = [s if i != 2 else (16, wide) for i, s in enumerate(sizes)]
        shape = lambda a, dtype: jax.ShapeDtypeStruct(a.shape, dtype)
        out_shape = (
            [shape(g, jnp.bfloat16) for g in grads[:6]]
            + [shape(grads[6], jnp.float32)]
            + [shape(w, jnp.float32) for w in weights]
            + [shape(w, jnp.float32) for w in weights]
        )
        scratch = [pltpu.VMEM((2,) * bits + s, jnp.float32) for s in sizes]
        for order, s in zip(orders, sizes):
            for step in range(bits):
                scratch.append(pltpu.VMEM((2,) * (bits - step - 1) + s, jnp.float32))
        scratch += [pltpu.VMEM((2,) * bits + s, jnp.bfloat16) for s in copy_sizes]
        scratch += [pltpu.SemaphoreType.DMA((len(sizes), 2 * bits))] * 2
        vmem = pl.BlockSpec(memory_space=pltpu.VMEM)
        outs = pl.pallas_call(
            functools.partial(kernel, n, bits, rows, orders),
            out_shape=out_shape,
            in_specs=[vmem] * 21,
            out_specs=[vmem] * 21,
            scratch_shapes=scratch,
            compiler_params=pltpu.CompilerParams(
                collective_id=0, has_side_effects=True, vmem_limit_bytes=60 * 2**20
            ),
        )(*grads, *weights, *moments)
        count = len(outs)
        anywhere = pl.BlockSpec(memory_space=pl.ANY)
        outs = pl.pallas_call(
            functools.partial(hand_on, count),
            out_shape=out_shape,
            in_specs=[anywhere] * count,
            out_specs=[anywhere] * count,
            scratch_shapes=[pltpu.VMEM(o.shape, o.dtype) for o in out_shape] + [pltpu.SemaphoreType.DMA((2, count))],
        )(*outs)
        outs = list(outs)
        for i in (2, 3, 4, 8, 15):
            outs[i] = outs[i].T
        outs[6] = outs[6].reshape(-1).astype(jnp.bfloat16)
        outs[13] = outs[13].reshape(-1)
        outs[20] = outs[20].reshape(-1)
        return tuple(outs)

    row, col, vec = P("data", "width"), P("width", "data"), P("data")
    part = (row, col, row, row, row, col, vec)
    return jax.shard_map(
        on_device,
        mesh=mesh,
        in_specs=(
            P("data", None, "width"),
            P("data", "width", None),
            P("data", None, "width"),
            P("data", None, "width"),
            P("data", None, "width"),
            P("data", "width", None),
            P("data", None),
        )
        + part
        + part,
        out_specs=(
            P(None, "width"),
            P("width", None),
            P(None, "width"),
            P(None, "width"),
            P(None, "width"),
            P("width", None),
            P(),
        )
        + part
        + part,
        check_vma=False,
    )
```

profile of v0, /device:TPU:0, one launch (start us, length us, event | category | flops | bytes accessed | tf_op | source)
XLA Modules:
  0.0 138.9 jit_solution(8651692964650177521)
XLA Ops:
  0.7 0.7 reduce
  1.4 0.7 reshape.59.refs_6_
  2.0 131.0 %shard_map.364 = (bf16[768,768]{1,0:T(8,128)(2,1)}, bf16[768,768]{1,0:T(8,128)(2,1)}, bf16[192,768]{1,0:T(8,128)(2,1)}, bf16[192,768]{1,0:T(8,128)(2,1)}, bf16[1...) custom-call(f32[768,768]{1,0:T(8,128)} %bitcast.23, ...), custom_call_target="tpu_custom_call" | custom-call | tf_op jit(solution)/shard_map/pallas_call | solution.py:325
  133.0 4.5 %shard_map.365 = (bf16[768,768]{1,0:T(8,128)(2,1)}, bf16[768,768]{1,0:T(8,128)(2,1)}, bf16[192,768]{1,0:T(8,128)(2,1)}, bf16[192,768]{1,0:T(8,128)(2,1)}, bf16[1...) custom-call(bf16[768,768]{1,0:T(8,128)(2,1)} %get-tuple-element.63.r, ...), custom_call_target="tpu_custom_call" | custom-call | tf_op jit(solution)/shard_map/pallas_call | solution.py:337
  137.5 0.7 convert_element_type.6
  138.2 0.7 convert_element_type.7
where the time goes:
time: 139 us
  Pallas kernels  136 us (98%)
    pallas_call x1, Pallas kernels, on_device(): pl.pallas_call(functools.partial(kernel, n, bits, rows, orders), out_shap...  131 us
    pallas_call x1, Pallas kernels, on_device(): pl.pallas_call(functools.partial(hand_on, count), out_shape=out_shape, in...  4.5 us

commit v1 on v0

v1 whole, which is shorter than its diff:
```python
import functools

import jax
import jax.numpy as jnp
from jax import lax
from jax.experimental import pallas as pl
from jax.experimental.pallas import tpu as pltpu
from jax.sharding import PartitionSpec as P

learn_rate = 0.05
hold_rate = 0.9
LANES = 128
SUB = 8
LOW, REACH = -125.0, 251.0
TINY = 1e-30


def round_up(value, unit):
    return -(-value // unit) * unit


def turn(block):
    rows, cols = block.shape
    tall, wide = round_up(rows, LANES), round_up(cols, LANES)
    if wide != cols:
        block = jnp.concatenate([block, jnp.zeros((rows, wide - cols), block.dtype)], axis=1)
    if tall != rows:
        block = jnp.concatenate([block, jnp.zeros((tall - rows, wide), block.dtype)], axis=0)
    return block.T[:cols, :rows]


def encode(x):
    limit = jnp.maximum(jnp.max(jnp.abs(x), axis=0, keepdims=True), TINY)
    size = jnp.exp2(jnp.abs(x) * (REACH / limit) + LOW)
    return jnp.where(x < 0.0, -size, size).astype(jnp.bfloat16), limit


def decode(code, limit):
    code = code.astype(jnp.float32)
    rate = limit * (1.0 / REACH)
    size = jnp.log2(jnp.abs(code)) * rate - LOW * rate
    return jnp.where(code < 0.0, -size, size)


def make_chunks(cols, heads):
    pieces = 3 if cols % (3 * LANES) == 0 else 1
    wide = cols // pieces
    up = [("up", i * wide, wide) for i in range(pieces)]
    down = [("down", i * wide, wide) for i in range(pieces)]
    first = [(up[0], True), (("vm", 0, 2 * heads), False)]
    rest = []
    for i in range(pieces):
        rest.append((down[i], i != 1))
        if i + 1 < pieces:
            rest.append((up[i + 1], i != 0))
    rest.insert(3, (("qk", 0, 2 * heads), True))
    return [c + (y, y) for c, y in first + rest]


def kernel(n, chunks, *refs):
    refs = list(refs)
    take = lambda count: [refs.pop(0) for _ in range(count)]
    grads = dict(zip(("up", "down", "query", "key", "value", "mixed", "norm"), take(7)))
    given = take(14)
    c_up, c_down, c_query, c_key, c_value, c_mixed, c_norm = take(7)
    n_up, n_down, n_query, n_key, n_value, n_mixed, n_norm = take(7)
    s_up, s_down, s_query, s_key, s_value, s_mixed, s_norm = take(7)
    near = take(14)
    w_up, w_down, w_query, w_key, w_value, w_mixed, w_norm = near[:7]
    m_up, m_down, m_query, m_key, m_value, m_mixed, m_norm = near[7:]
    count = len(chunks)
    L = n // 2
    raw = take(count)
    part = take(count)
    ysend = take(count)
    yhold = take(count)
    zsend = take(count)
    zhold = take(count)
    ysend_range, yhold_range, zsend_range, zhold_range = take(count), take(count), take(count), take(count)
    copies = take(count)
    g_norm, norm_hold, norm_copy = take(3)
    load_sem, y_sems, z_sems, ag_sems, ay_sems, norm_sems = take(6)

    rows = part[0].shape[-2]
    heads = w_query.shape[-1]
    mean_rate = n ** (-0.5)
    me = lax.axis_index("data")
    y, z = me % 2, me // 2
    other = 1 - y
    partner = me + 1 - 2 * y
    has_left, has_right = z > 0, z < L - 1

    def sources(chunk):
        kind, start, wide = chunks[chunk][:3]
        if kind == "up":
            return [(grads["up"].at[:, :, pl.ds(start, wide)], part[chunk])]
        if kind == "down":
            return [(grads["down"].at[pl.ds(start, wide)], raw[chunk])]
        pair = ("query", "key") if kind == "qk" else ("value", "mixed")
        return [(grads[p], raw[chunk].at[pl.ds(i * heads, heads)]) for i, p in enumerate(pair)]

    loads, small, at = [], [], 0
    for chunk in range(count):
        group = []
        for src, dst in sources(chunk):
            group.append(pltpu.make_async_copy(src, dst, load_sem.at[at]))
            at += 1
        loads.append(group)
    for src, dst in [(grads["norm"], g_norm)] + list(zip(given, near)):
        small.append(pltpu.make_async_copy(src, dst, load_sem.at[at]))
        at += 1
    for group in loads[:2]:
        for load in group:
            load.start()
    small[0].start()
    for group in loads[2:]:
        for load in group:
            load.start()
    for load in small[1:]:
        load.start()

    def start(copies):
        for copy in copies:
            copy.start()

    def wait_recv(copies):
        for copy in copies:
            copy.wait_recv()

    def wait_send(copies):
        for copy in copies:
            copy.wait_send()

    def remote(src, dst, sems, slot, there):
        return pltpu.make_async_remote_copy(
            src_ref=src,
            dst_ref=dst,
            send_sem=sems.at[(0,) + slot],
            recv_sem=sems.at[(1,) + slot],
            device_id={"data": there},
            device_id_type=pl.DeviceIdType.MESH,
        )

    barrier = pltpu.get_barrier_semaphore()
    for step in range(1, n):
        pl.semaphore_signal(
            barrier, inc=1, device_id={"data": (me + step) % n}, device_id_type=pl.DeviceIdType.MESH
        )

    def target(i):
        ahead = L - 1 - z
        far = jnp.where(i < ahead, L - 1 - i, i - ahead)
        back = jnp.where(i < z, i, L - 1 - (i - z))
        return jnp.where(2 * z < L, far, back)

    def y_first(chunk):
        return chunks[chunk][3]

    def y_last(chunk):
        return chunks[chunk][4]

    def prep(chunk):
        for load in loads[chunk]:
            load.wait()
        if chunks[chunk][0] == "up":
            return
        wide = chunks[chunk][2]
        for j in range(wide // LANES):
            block = turn(raw[chunk][j * LANES : (j + 1) * LANES, :])
            part[chunk][:, :, j * LANES : (j + 1) * LANES] = block.reshape(n, rows, LANES)

    def y_copy(chunk, slot):
        pairs = ((ysend, yhold), (ysend_range, yhold_range))
        return [
            remote(src[chunk].at[slot], dst[chunk].at[slot], y_sems, (k, chunk, slot), partner)
            for k, (src, dst) in enumerate(pairs)
        ]

    def y_value(chunk, slot):
        return decode(yhold[chunk][slot], yhold_range[chunk][slot])

    def y_code(chunk, slot, value):
        ysend[chunk][slot], ysend_range[chunk][slot] = encode(value)
        start(y_copy(chunk, slot))

    def start_y(chunk, i):
        t = z if i == L - 1 else target(i)
        y_code(chunk, t, part[chunk][2 * t + other])

    def z_copy(chunk, t):
        right = t > z
        there = jnp.where(right, z + 1, z - 1)
        slot = jnp.where(jnp.logical_and(t < z, t == z - 1), L, t)
        pairs = ((zsend, zhold), (zsend_range, zhold_range))
        return [
            pltpu.make_async_remote_copy(
                src_ref=src[chunk].at[t],
                dst_ref=dst[chunk].at[slot],
                send_sem=z_sems.at[0, k, chunk, t],
                recv_sem=z_sems.at[1, k, chunk, slot],
                device_id={"data": 2 * there + y},
                device_id_type=pl.DeviceIdType.MESH,
            )
            for k, (src, dst) in enumerate(pairs)
        ]

    def z_wait(chunk, slot):
        wait_recv(
            [
                remote(hold[chunk].at[slot], hold[chunk].at[slot], z_sems, (k, chunk, slot), partner)
                for k, hold in enumerate((zhold, zhold_range))
            ]
        )

    def z_value(chunk, slot, k):
        return decode(zhold[chunk][slot, k], zhold_range[chunk][slot, k])

    def step_z(chunk, i):
        t = target(i)
        held = jnp.logical_or(jnp.logical_and(t > z, has_left), jnp.logical_and(t < z, has_right))
        if y_first(chunk):
            wait_recv(y_copy(chunk, t))
            part[chunk][2 * t + y] = part[chunk][2 * t + y] + y_value(chunk, t)
            owners = (2 * t + y,)
        else:
            owners = (2 * t, 2 * t + 1)

        @pl.when(held)
        def _():
            z_wait(chunk, t)
            for k, owner in enumerate(owners):
                total = part[chunk][owner] + z_value(chunk, t, k)
                zsend[chunk][t, k], zsend_range[chunk][t, k] = encode(total)

        @pl.when(jnp.logical_not(held))
        def _():
            for k, owner in enumerate(owners):
                zsend[chunk][t, k], zsend_range[chunk][t, k] = encode(part[chunk][owner])

        start(z_copy(chunk, t))

    def add_held(chunk, owners):
        for k, owner in enumerate(owners):
            for there, slot in ((has_left, z), (has_right, L)):

                @pl.when(there)
                def _():
                    if k == 0:
                        z_wait(chunk, slot)
                    part[chunk][owner] = part[chunk][owner] + z_value(chunk, slot, k)

    def half_z(chunk):
        add_held(chunk, (2 * z, 2 * z + 1))
        y_code(chunk, 0, part[chunk][2 * z + other])

    def update(total, weight, moment):
        mean = total * mean_rate
        state = hold_rate * moment + (1.0 - hold_rate) * mean * mean
        return weight - learn_rate * mean * lax.rsqrt(state + 1e-06), state

    def finish(chunk):
        kind, start, wide = chunks[chunk][:3]
        if y_first(chunk):
            add_held(chunk, (me,))
        slot = z if y_first(chunk) else 0
        wait_recv(y_copy(chunk, slot))
        own = part[chunk][me] + y_value(chunk, slot)
        cols = slice(start, start + wide)
        if kind in ("up", "down"):
            weight, moment, new_out, state_out = (
                (w_up, m_up, n_up, s_up) if kind == "up" else (w_down, m_down, n_down, s_down)
            )
            new, state = update(own, weight[:, cols], moment[:, cols])
            copies[chunk][z, y] = new.astype(jnp.bfloat16)
            new_out[:, cols] = new
            state_out[:, cols] = state
        elif kind == "qk":
            weight = jnp.concatenate([w_query[...], w_key[...]], axis=1)
            moment = jnp.concatenate([m_query[...], m_key[...]], axis=1)
            new, state = update(own, weight, moment)
            copies[chunk][z, y] = new.astype(jnp.bfloat16)
            n_query[...], n_key[...] = new[:, :heads], new[:, heads:]
            s_query[...], s_key[...] = state[:, :heads], state[:, heads:]
        else:
            weight = jnp.concatenate([w_value[...], turn(w_mixed[...])], axis=1)
            moment = jnp.concatenate([m_value[...], turn(m_mixed[...])], axis=1)
            new, state = update(own, weight, moment)
            copies[chunk][z, y] = new.astype(jnp.bfloat16)
            n_value[...], s_value[...] = new[:, :heads], state[:, :heads]
            n_mixed[...] = turn(new[:, heads:])
            s_mixed[...] = turn(state[:, heads:])
        if y_last(chunk):
            spread(chunk, z, True, True)
            share(chunk, z).start()
        else:
            pair_copy(chunk).start()

    def pair_copy(chunk):
        spot = copies[chunk].at[z, y]
        return remote(spot, spot, ay_sems, (chunk, 0), partner)

    def share(chunk, s):
        spot = copies[chunk].at[s, y]
        return remote(spot, spot, ay_sems, (chunk, s), partner)

    def share_wait(chunk, s):
        spot = copies[chunk].at[s, other]
        remote(spot, spot, ay_sems, (chunk, s), partner).wait_recv()

    def line(chunk, s, right, slot):
        spot = copies[chunk].at[s, y] if y_last(chunk) else copies[chunk].at[s]
        there = z + 1 if right else z - 1
        return pltpu.make_async_remote_copy(
            src_ref=spot,
            dst_ref=spot,
            send_sem=ag_sems.at[0, chunk, slot],
            recv_sem=ag_sems.at[1, chunk, s],
            device_id={"data": 2 * there + y},
            device_id_type=pl.DeviceIdType.MESH,
        )

    def spread(chunk, s, right, left):
        if right:

            @pl.when(has_right)
            def _():
                line(chunk, s, True, s).start()

        if left:

            @pl.when(has_left)
            def _():
                line(chunk, s, False, L if right else s).start()

    def start_pair(chunk):
        spot = copies[chunk].at[z, other]
        remote(spot, spot, ay_sems, (chunk, 0), partner).wait_recv()
        spread(chunk, z, True, True)

    def hop(chunk, h):
        for right in (True, False):
            s = z - h if right else z + h

            @pl.when(s >= 0 if right else s < L)
            def _():
                line(chunk, s, right, s).wait_recv()
                spread(chunk, s, right, not right)
                if y_last(chunk):
                    share(chunk, s).start()

    def drain_reduce(chunk):
        for t in range(L if y_first(chunk) else 1):
            wait_send(y_copy(chunk, t))
        for i in range(L - 1):
            wait_send(z_copy(chunk, target(i)))

    def drain_gather(chunk):
        if y_last(chunk):
            for s in range(L):
                share(chunk, s).wait_send()
        else:
            pair_copy(chunk).wait_send()

        @pl.when(has_right)
        def _():
            line(chunk, z, True, z).wait_send()

        @pl.when(has_left)
        def _():
            line(chunk, z, False, L).wait_send()

        for h in range(1, L):

            @pl.when(jnp.logical_and(z - h >= 0, has_right))
            def _():
                line(chunk, z - h, True, z - h).wait_send()

            @pl.when(jnp.logical_and(z + h < L, has_left))
            def _():
                line(chunk, z + h, False, z + h).wait_send()

    group = 1 if rows % 16 == 0 else 2

    def end(chunk):
        kind, start, wide = chunks[chunk][:3]
        if y_last(chunk):
            for s in range(L):
                share_wait(chunk, s)
        if kind == "up":
            for d in range(0, n, group):
                got = [copies[chunk][(d + i) // 2, (d + i) % 2] for i in range(group)]
                if group > 1:
                    got = [jnp.concatenate([g.astype(jnp.float32) for g in got], axis=0).astype(jnp.bfloat16)]
                c_up[d * rows : (d + group) * rows, start : start + wide] = got[0]
            return
        for j in range(wide // LANES):
            value = copies[chunk][:, :, :, j * LANES : (j + 1) * LANES].astype(jnp.float32)
            value = turn(value.reshape(n * rows, LANES)).astype(jnp.bfloat16)
            if kind == "down":
                c_down[start + j * LANES : start + (j + 1) * LANES, :] = value
                continue
            first, second = (c_query, c_key) if kind == "qk" else (c_value, c_mixed)
            done = 0
            while done < LANES:
                at = j * LANES + done
                out, base = (first, 0) if at < heads else (second, heads)
                size = min(LANES - done, heads + base - at)
                out[at - base : at - base + size, :] = value[done : done + size]
                done += size

    def norm_copies(give):
        src, dst = (g_norm, norm_hold) if give else (norm_copy.at[me], norm_copy)
        return [
            remote(src, dst.at[me], norm_sems, (0 if give else 1, step), (me + step) % n) for step in range(1, n)
        ]

    def norm_arrivals(give):
        hold = norm_hold if give else norm_copy
        for step in range(1, n):
            spot = hold.at[(me + n - step) % n]
            remote(spot, spot, norm_sems, (0 if give else 1, step), partner).wait_recv()

    def norm_start():
        small[0].wait()
        norm_hold[me] = g_norm[...]
        for copy in norm_copies(True):
            copy.start()

    def norm_update():
        norm_arrivals(True)
        total = norm_hold[0]
        for d in range(1, n):
            total = total + norm_hold[d]
        own = total[:, :rows]
        for d in range(1, n):
            own = jnp.where(me == d, total[:, d * rows : (d + 1) * rows], own)
        new, state = update(own, w_norm[...], m_norm[...])
        n_norm[...] = new
        s_norm[...] = state
        wide = norm_copy.shape[-1]
        if wide != rows:
            new = jnp.concatenate([new, jnp.zeros((1, wide - rows), jnp.float32)], axis=1)
        norm_copy[me] = new
        for copy in norm_copies(False):
            copy.start()

    def norm_end():
        norm_arrivals(False)
        got = [norm_copy[d][:, :rows] for d in range(n)]
        c_norm[...] = jnp.concatenate(got, axis=1)
        for give in (True, False):
            for copy in norm_copies(give):
                copy.wait_send()

    def smalls():
        for load in small[1:]:
            load.wait()

    events = []
    add = lambda time, body, *args: events.append((time, len(events), body, args))
    gap, hop_time = 4.0, 2.5
    for chunk in range(count):
        time = gap * chunk
        add(time, prep, chunk)
        if y_first(chunk):
            for i in range(L):
                add(time, start_y, chunk, i)
            time += hop_time
        for i in range(L - 1):
            add(time + hop_time * min(i, L // 2), step_z, chunk, i)
        time += hop_time * (L - 1)
        if not y_first(chunk):
            add(time, half_z, chunk)
            time += hop_time
        add(time, finish, chunk)
        if not y_last(chunk):
            time += hop_time
            add(time, start_pair, chunk)
        for h in range(1, L):
            time += hop_time
            add(time, hop, chunk, h)
        add(time, drain_reduce, chunk)
        if y_last(chunk):
            time += hop_time
        add(time, end, chunk)
        add(time + 2 * hop_time, drain_gather, chunk)
    add(gap + 0.1, norm_start)
    add(2 * hop_time, smalls)
    add(gap * 2 + 2 * hop_time, norm_update)
    add(gap * 4 + 2 * hop_time, norm_end)
    events.sort(key=lambda e: e[:2])

    barrier_done = False
    for _, _, body, args in events:
        if body is not prep and not barrier_done:
            pl.semaphore_wait(barrier, n - 1)
            barrier_done = True
        body(*args)


def hand_on(count, *refs):
    given, out, sem = refs[:count], refs[count : 2 * count], refs[2 * count]
    writes = [pltpu.make_async_copy(given[i], out[i], sem.at[i]) for i in range(count)]
    for write in writes:
        write.start()
    for write in writes:
        write.wait()


def solution(mesh):
    n = mesh.shape["data"]
    L = n // 2

    def on_device(*args):
        grads, weights, moments = args[:7], args[7:14], args[14:]
        rows = weights[0].shape[0]
        cols = grads[0].shape[2]
        grads = [g[0].T if i in (2, 3, 4) else g[0] for i, g in enumerate(grads[:6])] + [grads[6]]
        grads[0] = grads[0].reshape(n, rows, cols)
        heads = grads[2].shape[0]
        weights = list(weights[:6]) + [weights[6].reshape(1, rows)]
        moments = list(moments[:6]) + [moments[6].reshape(1, rows)]
        weights[1], moments[1] = weights[1].T, moments[1].T
        chunks = make_chunks(cols, heads)
        count = len(chunks)
        wide_norm = round_up(rows, LANES)
        copy_shapes = [(n * rows, cols), grads[1].shape] + [g.shape for g in grads[2:6]]
        out_shape = (
            [pltpu.VMEM(s, jnp.bfloat16) for s in copy_shapes]
            + [pltpu.VMEM((1, n * rows), jnp.float32)]
            + [pltpu.VMEM(w.shape, jnp.float32) for w in weights] * 2
        )
        scratch = [pltpu.VMEM(w.shape, jnp.float32) for w in weights + moments]
        bf16 = jnp.bfloat16
        scratch += [pltpu.VMEM((c[2], n * rows) if c[0] != "up" else (SUB, LANES), jnp.float32) for c in chunks]
        scratch += [pltpu.VMEM((n, rows, c[2]), jnp.float32) for c in chunks]
        for tall, dtype in ((rows, bf16), (1, jnp.float32)):
            for _ in range(2):
                scratch += [pltpu.VMEM((L if c[3] else 1, tall, c[2]), dtype) for c in chunks]
            for slots in (L, L + 1):
                scratch += [pltpu.VMEM((slots, 1 if c[3] else 2, tall, c[2]), dtype) for c in chunks]
        scratch += [pltpu.VMEM((L, 2, rows, c[2]), bf16) for c in chunks]
        scratch += [
            pltpu.VMEM((1, n * rows), jnp.float32),
            pltpu.VMEM((n, 1, n * rows), jnp.float32),
            pltpu.VMEM((n, 1, wide_norm), jnp.float32),
        ]
        sem = pltpu.SemaphoreType.DMA
        scratch += [
            sem((2 * count + 15,)),
            sem((2, 2, count, L)),
            sem((2, 2, count, L + 1)),
            sem((2, count, L + 1)),
            sem((2, count, L)),
            sem((2, 2, n)),
        ]
        anywhere = pl.BlockSpec(memory_space=pl.ANY)
        vmem = pl.BlockSpec(memory_space=pltpu.VMEM)
        with jax.sharding.use_abstract_mesh(mesh.abstract_mesh):
            outs = pl.pallas_call(
                functools.partial(kernel, n, chunks),
                out_shape=out_shape,
                in_specs=[anywhere] * 21,
                out_specs=[vmem] * 21,
                scratch_shapes=scratch,
                compiler_params=pltpu.CompilerParams(
                    collective_id=0, has_side_effects=True, vmem_limit_bytes=48 * 2**20
                ),
            )(*grads, *weights, *moments)
            total = len(outs)
            outs = pl.pallas_call(
                functools.partial(hand_on, total),
                out_shape=[jax.ShapeDtypeStruct(o.shape, o.dtype) for o in out_shape],
                in_specs=[vmem] * total,
                out_specs=[anywhere] * total,
                scratch_shapes=[sem((total,))],
                compiler_params=pltpu.CompilerParams(vmem_limit_bytes=2**20),
            )(*outs)
        outs = list(outs)
        for i in (2, 3, 4, 8, 15):
            outs[i] = outs[i].T
        outs[6] = outs[6].reshape(-1).astype(jnp.bfloat16)
        outs[13] = outs[13].reshape(-1)
        outs[20] = outs[20].reshape(-1)
        return tuple(outs)

    row, col, vec = P("data", "width"), P("width", "data"), P("data")
    part = (row, col, row, row, row, col, vec)
    return jax.shard_map(
        on_device,
        mesh=mesh,
        in_specs=(
            P("data", None, "width"),
            P("data", "width", None),
            P("data", None, "width"),
            P("data", None, "width"),
            P("data", None, "width"),
            P("data", "width", None),
            P("data", None),
        )
        + part
        + part,
        out_specs=(
            P(None, "width"),
            P("width", None),
            P(None, "width"),
            P(None, "width"),
            P(None, "width"),
            P("width", None),
            P(),
        )
        + part
        + part,
        check_vma=False,
    )
```

time: 139 us -> 117 us (0.84)
  Pallas kernels: 136 us -> 107 us
  local copies, waits for them, and re-layouts: 1.33 us -> 8.23 us
    pallas_call x2, Pallas kernels: 136 us -> 107 us  [the longest x1 104 us: on_device(): pl.pallas_call(functools.partial(kernel, n, chunks), out_shape=out_shape,...]
    unnamed x0 -> x20, local copies, waits for them, and re-layouts: none -> 8.23 us
where the time goes in v1:
time: 117 us
  Pallas kernels  107 us (91%)
  local copies, waits for them, and re-layouts  8.23 us (7%)
    pallas_call x1, Pallas kernels, on_device(): pl.pallas_call(functools.partial(kernel, n, chunks), out_shape=out_shape,...  104 us
    unnamed x20, local copies, waits for them, and re-layouts  8.23 us
    pallas_call x1, Pallas kernels, on_device(): pl.pallas_call(functools.partial(hand_on, total), out_shape=[jax.ShapeDty...  2.63 us

profile of v1, /device:TPU:0, one launch (start us, length us, event | category | flops | bytes accessed | tf_op | source)
XLA Modules:
  0.0 116.6 jit_solution(15339809825102218571)
XLA Ops:
  0.7 0.0 copy-start
  0.7 0.9 copy-done
  1.6 0.0 copy-start.1
  1.6 0.9 copy-done.1
  2.5 0.0 copy-start.2
  2.5 0.9 copy-done.2
  3.3 0.0 copy-start.3
  3.3 0.9 copy-done.3
  4.2 0.0 copy-start.4
  4.2 0.9 copy-done.4
  5.1 0.0 copy-start.5
  5.1 0.9 copy-done.5
  6.0 0.0 copy-start.6
  6.0 0.9 copy-done.6
  6.9 0.0 copy-start.7
  6.9 0.7 copy-done.7
  7.6 0.0 copy-start.8
  7.6 0.7 copy-done.8
  8.3 0.0 copy-start.9
  8.3 0.7 copy-done.9
  8.9 104.5 %shard_map.364 = (bf16[768,768]{1,0:T(8,128)(2,1)S(1)}, bf16[768,768]{1,0:T(8,128)(2,1)S(1)}, bf16[192,768]{1,0:T(8,128)(2,1)S(1)}, bf16[192,768]{1,0:T(8,128)(2...) custom-call(f32[8,96,768]{2,1,0:T(8,128)} %bitcast.25, ...), custom_call_target="tpu_custom_call" | custom-call | tf_op jit(solution)/shard_map/pallas_call | solution.py:560
  113.4 2.6 %shard_map.365 = (bf16[768,768]{1,0:T(8,128)(2,1)}, bf16[768,768]{1,0:T(8,128)(2,1)}, bf16[192,768]{1,0:T(8,128)(2,1)}, bf16[192,768]{1,0:T(8,128)(2,1)}, bf16[1...) custom-call(bf16[768,768]{1,0:T(8,128)(2,1)S(1)} %get-tuple-element., ...), custom_call_target="tpu_custom_call" | custom-call | tf_op jit(solution)/shard_map/pallas_call | solution.py:571
  116.0 0.6 convert_reduce_fusion
Async XLA Ops:
  0.7 0.9 copy-start
  1.6 0.9 copy-start.1
  2.5 0.9 copy-start.2
  3.3 0.9 copy-start.3
  4.2 0.9 copy-start.4
  5.1 0.9 copy-start.5
  6.0 0.9 copy-start.6
  6.9 0.7 copy-start.7
  7.6 0.7 copy-start.8
  8.3 0.7 copy-start.9

commit v2 on v1

v2 whole, which is shorter than its diff:
```python
import functools

import jax
import jax.numpy as jnp
from jax import lax
from jax.experimental import pallas as pl
from jax.experimental.pallas import tpu as pltpu
from jax.sharding import PartitionSpec as P

learn_rate = 0.05
hold_rate = 0.9
LANES = 128
SUB = 8
LOW, REACH = -125.0, 251.0
TINY = 1e-30


PLAN = [
    ("up", 2, 0),
    ("up", 2, 1),
    ("down", 2, 1),
    ("down", 2, 1),
    ("vm", 1, 0),
    ("qk", 3, 1),
    ("vm", 2, 1),
    ("down", 2, 0),
    ("up", 2, 1),
]
ORDERS = [
    [
        (0, 0, 0), (2, 0, 0), (2, 0, 1), (0, 2, 0), (1, 2, 0), (1, 2, 2), (0, 4, 0), (0, 1, 0),
        (2, 4, 0), (1, 1, 0), (0, 3, 0), (0, 5, 0), (2, 2, 0), (1, 2, 1), (1, 1, 1), (1, 3, 2),
        (2, 1, 0), (1, 3, 1), (1, 3, 0), (1, 1, 3), (1, 1, 2), (1, 5, 0), (2, 0, 2), (1, 5, 2),
        (2, 2, 1), (1, 5, 1), (1, 2, 3), (2, 4, 1), (2, 1, 1), (0, 8, 0), (0, 6, 0), (1, 8, 3),
        (2, 3, 0), (2, 2, 2), (2, 3, 1), (1, 3, 3), (0, 7, 0), (2, 1, 2), (4, 1, 0), (3, 0, 0),
        (1, 8, 2), (2, 3, 2), (2, 5, 0), (2, 5, 1), (1, 6, 1), (2, 4, 2), (2, 7, 0), (1, 6, 0),
        (3, 4, 0), (4, 2, 0), (1, 8, 0), (4, 0, 0), (1, 6, 2), (2, 5, 2), (6, 2, -2), (6, 3, -1),
        (2, 7, 1), (2, 6, 0), (1, 5, 3), (6, 1, -1), (1, 8, 1), (5, 0, 0), (2, 6, 1), (2, 7, 2),
        (2, 8, 0), (6, 5, -1), (4, 4, 0), (4, 3, 0), (1, 6, 3), (5, 4, 0), (3, 7, 0), (6, 1, -3),
        (2, 6, 2), (6, 2, -3), (4, 5, 0), (6, 0, -3), (2, 8, 1), (6, 2, -1), (6, 3, -2), (4, 6, 0),
        (6, 0, -2), (4, 7, 0), (2, 8, 2), (6, 3, -3), (6, 5, -2), (4, 8, 0), (6, 6, -1), (6, 1, -2),
        (5, 7, 0), (6, 7, -1), (6, 4, -1), (6, 6, -2), (6, 0, -1), (7, 3, 0), (6, 8, -1), (7, 1, 0),
        (6, 5, -3), (7, 0, 0), (6, 4, -3), (7, 2, 0), (6, 6, -3), (6, 8, -2), (6, 8, -3), (7, 5, 0),
        (6, 4, -2), (7, 6, 0), (7, 4, 0), (7, 8, 0), (6, 7, -2), (6, 7, -3), (7, 7, 0),
    ],
    [
        (0, 1, 0), (1, 1, 1), (0, 0, 0), (0, 3, 0), (1, 1, 3), (1, 1, 2), (0, 2, 0), (0, 5, 0),
        (1, 2, 0), (1, 3, 0), (1, 2, 1), (1, 1, 0), (2, 0, 0), (0, 6, 0), (1, 2, 3), (2, 0, 1),
        (0, 4, 0), (1, 3, 2), (2, 2, 0), (1, 2, 2), (2, 1, 0), (1, 3, 1), (2, 0, 2), (1, 5, 0),
        (2, 4, 0), (1, 6, 2), (3, 0, 0), (2, 1, 2), (2, 2, 1), (1, 3, 3), (2, 2, 2), (0, 7, 0),
        (2, 1, 1), (2, 4, 2), (2, 3, 0), (1, 5, 3), (1, 5, 2), (4, 2, 0), (2, 3, 1), (4, 0, 0),
        (1, 5, 1), (2, 4, 1), (2, 3, 2), (6, 1, 1), (4, 1, 0), (6, 2, -1), (4, 3, 0), (2, 5, 0),
        (5, 0, 0), (6, 1, -2), (0, 8, 0), (1, 6, 0), (3, 4, 0), (2, 5, 1), (6, 1, -1), (2, 5, 2),
        (6, 0, -1), (6, 2, 1), (2, 7, 0), (4, 5, 0), (2, 7, 1), (4, 4, 0), (6, 3, -1), (1, 6, 1),
        (6, 2, -2), (2, 7, 2), (1, 8, 0), (6, 0, 1), (2, 6, 0), (6, 5, -1), (2, 6, 1), (3, 7, 0),
        (1, 6, 3), (5, 4, 0), (6, 0, -2), (2, 8, 0), (2, 6, 2), (6, 3, 1), (1, 8, 2), (6, 4, 1),
        (6, 4, -1), (7, 0, 0), (1, 8, 1), (4, 7, 0), (4, 6, 0), (1, 8, 3), (6, 5, 1), (6, 3, -2),
        (2, 8, 2), (6, 6, -1), (2, 8, 1), (6, 4, -2), (6, 6, 1), (5, 7, 0), (4, 8, 0), (6, 5, -2),
        (7, 4, 0), (6, 6, -2), (6, 8, 1), (6, 8, -1), (6, 7, 1), (6, 8, -2), (6, 7, -1), (7, 2, 0),
        (7, 3, 0), (6, 7, -2), (7, 7, 0), (7, 8, 0), (7, 1, 0), (7, 6, 0), (7, 5, 0),
    ],
]


def round_up(value, unit):
    return -(-value // unit) * unit


def turn(block):
    rows, cols = block.shape
    tall, wide = round_up(rows, LANES), round_up(cols, LANES)
    if wide != cols:
        block = jnp.concatenate([block, jnp.zeros((rows, wide - cols), block.dtype)], axis=1)
    if tall != rows:
        block = jnp.concatenate([block, jnp.zeros((tall - rows, wide), block.dtype)], axis=0)
    return block.T[:cols, :rows]


def encode(x):
    limit = jnp.maximum(jnp.max(jnp.abs(x), axis=0, keepdims=True), TINY)
    size = jnp.exp2(jnp.abs(x) * (REACH / limit) + LOW)
    return jnp.where(x < 0.0, -size, size).astype(jnp.bfloat16), limit


def decode(code, limit):
    code = code.astype(jnp.float32)
    rate = limit * (1.0 / REACH)
    size = jnp.log2(jnp.abs(code)) * rate - LOW * rate
    return jnp.where(code < 0.0, -size, size)


PREP, START, STEP, HALF, FINISH, PAIR, HOP, END = range(8)


def make_chunks(cols, heads, plan):
    room = {"up": cols, "down": cols, "vm": 2 * heads, "qk": 2 * heads}
    if sum(room.values()) != LANES * sum(p[1] for p in plan):
        plan = [("up", cols // LANES, 1), ("vm", 2 * heads // LANES, 0), ("down", cols // LANES, 1)]
        plan += [("qk", 2 * heads // LANES, 0)]
    at = dict.fromkeys(room, 0)
    chunks = []
    for kind, tiles, y_first in plan:
        chunks.append((kind, at[kind], tiles * LANES, bool(y_first)))
        at[kind] += tiles * LANES
    return chunks


def plain_order(L, chunks):
    events = []
    for c, (_, _, _, y_first) in enumerate(chunks):
        time = 4 * c

        def add(kind, arg=0):
            events.append((time, len(events), (kind, c, arg)))

        add(PREP)
        if y_first:
            for i in range(L):
                add(START, i)
            time += 4
        for i in range(L - 1):
            add(STEP, i)
            time += 2
        if not y_first:
            add(HALF)
            time += 4
        add(FINISH)
        if not y_first:
            time += 4
            add(PAIR)
        for h in range(1, L):
            time += 4
            add(HOP, h)
            add(HOP, -h)
        time += 4
        add(END)
    return [e[2] for e in sorted(events)]


def pick(cond, one, two):
    if isinstance(cond, bool):
        return one if cond else two
    return jnp.where(cond, one, two)


def when(cond, body):
    if not isinstance(cond, bool):
        pl.when(cond)(body)
    elif cond:
        body()


def start(copies):
    for copy in copies:
        copy.start()


def wait_recv(copies):
    for copy in copies:
        copy.wait_recv()


def wait_send(copies):
    for copy in copies:
        copy.wait_send()


def remote(src, dst, sems, send_slot, recv_slot, there):
    return pltpu.make_async_remote_copy(
        src_ref=src,
        dst_ref=dst,
        send_sem=sems.at[(0,) + send_slot],
        recv_sem=sems.at[(1,) + recv_slot],
        device_id={"data": there},
        device_id_type=pl.DeviceIdType.MESH,
    )


def update(total, weight, moment, mean_rate):
    mean = total * mean_rate
    state = hold_rate * moment + (1.0 - hold_rate) * mean * mean
    return weight - learn_rate * mean * lax.rsqrt(state + 1e-06), state


def kernel(n, chunks, orders, *refs):
    refs = list(refs)
    take = lambda count: [refs.pop(0) for _ in range(count)]
    grads = dict(zip(("up", "down", "query", "key", "value", "mixed", "norm"), take(7)))
    given = take(14)
    c_up, c_down, c_query, c_key, c_value, c_mixed, c_norm = take(7)
    n_up, n_down, n_query, n_key, n_value, n_mixed, n_norm = take(7)
    s_up, s_down, s_query, s_key, s_value, s_mixed, s_norm = take(7)
    near = take(14)
    w_up, w_down, w_query, w_key, w_value, w_mixed, w_norm = near[:7]
    m_up, m_down, m_query, m_key, m_value, m_mixed, m_norm = near[7:]
    pair = {kind: take(4) for kind in ("qk", "vm")}
    count = len(chunks)
    L = n // 2
    raw = take(count)
    part = take(count)
    ysend = take(count)
    yhold = take(count)
    zsend = take(count)
    zhold = take(count)
    ysend_range, yhold_range, zsend_range, zhold_range = take(count), take(count), take(count), take(count)
    copies = take(count)
    g_norm, norm_hold, norm_copy = take(3)
    load_sem, y_sems, z_sems, ag_sems, ay_sems, norm_sems = take(6)

    rows = part[0].shape[-2]
    heads = w_query.shape[-1]
    mean_rate = n ** (-0.5)
    me = lax.axis_index("data")
    y, z = me % 2, me // 2
    other = 1 - y
    partner = me + 1 - 2 * y

    loads, small, at = [], [], 0
    for chunk, (kind, first, wide, _) in enumerate(chunks):
        if kind == "up":
            moves = [(grads["up"].at[:, :, pl.ds(first, wide)], part[chunk])]
        elif kind == "down":
            moves = [(grads["down"].at[pl.ds(first, wide)], raw[chunk])]
        else:
            moves = []
            for k, name in enumerate(("query", "key") if kind == "qk" else ("value", "mixed")):
                low, high = max(first, k * heads), min(first + wide, (k + 1) * heads)
                if low < high:
                    src = grads[name].at[pl.ds(low - k * heads, high - low)]
                    moves.append((src, raw[chunk].at[pl.ds(low - first, high - low)]))
        group = []
        for src, dst in moves:
            group.append(pltpu.make_async_copy(src, dst, load_sem.at[at]))
            at += 1
        loads.append(group)
    for src, dst in [(grads["norm"], g_norm)] + list(zip(given, near)):
        small.append(pltpu.make_async_copy(src, dst, load_sem.at[at]))
        at += 1
    for k, group in enumerate(loads):
        start(group)
        if k == 1:
            start(small[:1])
    start(small[1:])

    barrier = pltpu.get_barrier_semaphore()
    for step in range(1, n):
        pl.semaphore_signal(
            barrier, inc=1, device_id={"data": (me + step) % n}, device_id_type=pl.DeviceIdType.MESH
        )

    def norm_copies(give):
        src, dst = (g_norm, norm_hold) if give else (norm_copy.at[me], norm_copy)
        sets = [((0 if give else 1, step), (me + step) % n) for step in range(1, n)]
        return [remote(src, dst.at[me], norm_sems, slot, slot, there) for slot, there in sets]

    def norm_arrivals(give):
        hold = norm_hold if give else norm_copy
        for step in range(1, n):
            spot, slot = hold.at[(me + n - step) % n], (0 if give else 1, step)
            remote(spot, spot, norm_sems, slot, slot, partner).wait_recv()

    def norm_start():
        small[0].wait()
        norm_hold[me] = g_norm[...]
        start(norm_copies(True))

    def norm_update():
        norm_arrivals(True)
        total = norm_hold[0]
        for d in range(1, n):
            total = total + norm_hold[d]
        own = total[:, :rows]
        for d in range(1, n):
            own = jnp.where(me == d, total[:, d * rows : (d + 1) * rows], own)
        new, state = update(own, w_norm[...], m_norm[...], mean_rate)
        n_norm[...] = new
        s_norm[...] = state
        wide = norm_copy.shape[-1]
        if wide != rows:
            new = jnp.concatenate([new, jnp.zeros((1, wide - rows), jnp.float32)], axis=1)
        norm_copy[me] = new
        start(norm_copies(False))

    def norm_end():
        norm_arrivals(False)
        got = [norm_copy[d][:, :rows] for d in range(n)]
        c_norm[...] = jnp.concatenate(got, axis=1)
        for give in (True, False):
            wait_send(norm_copies(give))

    def smalls():
        for load in small[1:]:
            load.wait()
        pair["qk"][0][...] = jnp.concatenate([w_query[...], w_key[...]], axis=1)
        pair["qk"][1][...] = jnp.concatenate([m_query[...], m_key[...]], axis=1)
        pair["vm"][0][...] = jnp.concatenate([w_value[...], turn(w_mixed[...])], axis=1)
        pair["vm"][1][...] = jnp.concatenate([m_value[...], turn(m_mixed[...])], axis=1)

    def pairs_end(kind):
        new, state = pair[kind][2][...], pair[kind][3][...]
        if kind == "qk":
            n_query[...], n_key[...] = new[:, :heads], new[:, heads:]
            s_query[...], s_key[...] = state[:, :heads], state[:, heads:]
        else:
            n_value[...], s_value[...] = new[:, :heads], state[:, :heads]
            n_mixed[...], s_mixed[...] = turn(new[:, heads:]), turn(state[:, heads:])

    group = 1 if rows % 16 == 0 else 2

    def program(order, zm, mirror):
        forward = 1 - 2 * mirror
        real = lambda place: mirror * (L - 1) + forward * place
        has_near, has_far = zm > 0, zm < L - 1
        from_near, from_far = z + mirror * (L - z), z + (1 - mirror) * (L - z)

        def target(i):
            ahead = L - 1 - zm
            far = pick(i < ahead, L - 1 - i, i - ahead)
            back = pick(i < zm, i, L - 1 - (i - zm))
            return pick(2 * zm < L, far, back)

        def y_copy(chunk, slot):
            pairs = ((ysend, yhold), (ysend_range, yhold_range))
            return [
                remote(src[chunk].at[slot], dst[chunk].at[slot], y_sems, (k, chunk, slot), (k, chunk, slot), partner)
                for k, (src, dst) in enumerate(pairs)
            ]

        def y_value(chunk, slot):
            return decode(yhold[chunk][slot], yhold_range[chunk][slot])

        def y_code(chunk, slot, value):
            ysend[chunk][slot], ysend_range[chunk][slot] = encode(value)
            start(y_copy(chunk, slot))

        def z_copy(chunk, place):
            ahead = place > zm
            there, t = pick(ahead, zm + 1, zm - 1), real(place)
            leftward = pick(ahead, mirror, 1 - mirror)
            slot = pick(there == place, t + leftward * (L - t), t)
            pairs = ((zsend, zhold), (zsend_range, zhold_range))
            return [
                remote(
                    src[chunk].at[t],
                    dst[chunk].at[slot],
                    z_sems,
                    (k, chunk, t),
                    (k, chunk, slot),
                    2 * real(there) + y,
                )
                for k, (src, dst) in enumerate(pairs)
            ]

        def z_wait(chunk, slot):
            for k, hold in enumerate((zhold, zhold_range)):
                spot = hold[chunk].at[slot]
                remote(spot, spot, z_sems, (k, chunk, slot), (k, chunk, slot), partner).wait_recv()

        def z_value(chunk, slot, k):
            return decode(zhold[chunk][slot, k], zhold_range[chunk][slot, k])

        def prep(chunk, _):
            for load in loads[chunk]:
                load.wait()
            if chunks[chunk][0] == "up":
                return
            for j in range(chunks[chunk][2] // LANES):
                block = turn(raw[chunk][j * LANES : (j + 1) * LANES, :])
                part[chunk][:, :, j * LANES : (j + 1) * LANES] = block.reshape(n, rows, LANES)

        def start_y(chunk, i):
            t = z if i == L - 1 else real(target(i))
            y_code(chunk, t, part[chunk][2 * t + other])

        def step_z(chunk, i):
            place = target(i)
            t = real(place)
            held = pick(place > zm, has_near, has_far)
            if chunks[chunk][3]:
                wait_recv(y_copy(chunk, t))
                owners = (2 * t + y,)
            else:
                owners = (2 * t, 2 * t + 1)

            def own(owner):
                value = part[chunk][owner]
                return value + y_value(chunk, t) if chunks[chunk][3] else value

            def with_held():
                z_wait(chunk, t)
                for k, owner in enumerate(owners):
                    total = own(owner) + z_value(chunk, t, k)
                    zsend[chunk][t, k], zsend_range[chunk][t, k] = encode(total)

            def without():
                for k, owner in enumerate(owners):
                    zsend[chunk][t, k], zsend_range[chunk][t, k] = encode(own(owner))

            when(held, with_held)
            when((not held) if isinstance(held, bool) else jnp.logical_not(held), without)
            start(z_copy(chunk, place))

        def add_held(chunk, owners):
            for there, slot in ((has_near, from_near), (has_far, from_far)):

                def body():
                    z_wait(chunk, slot)
                    for k, owner in enumerate(owners):
                        part[chunk][owner] = part[chunk][owner] + z_value(chunk, slot, k)

                when(there, body)

        def half_z(chunk, _):
            add_held(chunk, (2 * z, 2 * z + 1))
            y_code(chunk, 0, part[chunk][2 * z + other])

        def finish(chunk, _):
            kind, first, wide, y_first = chunks[chunk]
            if y_first:
                add_held(chunk, (me,))
            slot = z if y_first else 0
            wait_recv(y_copy(chunk, slot))
            total = part[chunk][me] + y_value(chunk, slot)
            if kind == "up":
                weight, moment, new_out, state_out = w_up, m_up, n_up, s_up
            elif kind == "down":
                weight, moment, new_out, state_out = w_down, m_down, n_down, s_down
            else:
                weight, moment, new_out, state_out = pair[kind]
            cols = slice(first, first + wide)
            new, state = update(total, weight[:, cols], moment[:, cols], mean_rate)
            copies[chunk][z, y] = new.astype(jnp.bfloat16)
            if y_first:
                spread(chunk, z, True, True)
                share(chunk, z).start()
            else:
                whole(chunk, y).start()
            new_out[:, cols] = new
            state_out[:, cols] = state

        def whole(chunk, side):
            spot = copies[chunk].at[z, side]
            return remote(spot, spot, ay_sems, (chunk, 0), (chunk, 0), partner)

        def share(chunk, s, side=y):
            spot = copies[chunk].at[s, side]
            return remote(spot, spot, ay_sems, (chunk, s), (chunk, s), partner)

        def line(chunk, s, ahead, slot):
            spot = copies[chunk].at[s, y] if chunks[chunk][3] else copies[chunk].at[s]
            there = 2 * real(zm + 1 if ahead else zm - 1) + y
            return remote(spot, spot, ag_sems, (chunk, slot), (chunk, s), there)

        def spread(chunk, s, far, close):
            if far:
                when(has_far, lambda: line(chunk, s, True, s).start())
            if close:
                when(has_near, lambda: line(chunk, s, False, L if far else s).start())

        def start_pair(chunk, _):
            whole(chunk, other).wait_recv()
            spread(chunk, z, True, True)

        def hop(chunk, h):
            place = zm - h

            def body():
                s = real(place)
                line(chunk, s, h > 0, s).wait_recv()
                spread(chunk, s, h > 0, h < 0)
                if chunks[chunk][3]:
                    share(chunk, s).start()

            when(place >= 0 if h > 0 else place < L, body)

        def drain(chunk):
            y_first = chunks[chunk][3]
            for t in range(L if y_first else 1):
                wait_send(y_copy(chunk, t))
            for i in range(L - 1):
                wait_send(z_copy(chunk, target(i)))
            if y_first:
                for s in range(L):
                    share(chunk, s).wait_send()
            else:
                whole(chunk, y).wait_send()
            when(has_far, lambda: line(chunk, z, True, z).wait_send())
            when(has_near, lambda: line(chunk, z, False, L).wait_send())
            for h in range(1, L):
                for place, ahead, on in ((zm - h, True, has_far), (zm + h, False, has_near)):
                    inside = place >= 0 if ahead else place < L
                    both = (inside and on) if isinstance(on, bool) else jnp.logical_and(inside, on)
                    when(both, lambda: line(chunk, real(place), ahead, real(place)).wait_send())

        def end(chunk, _):
            kind, first, wide, y_first = chunks[chunk]
            if y_first:
                for s in range(L):
                    share(chunk, s, other).wait_recv()
            if kind == "up":
                for d in range(0, n, group):
                    got = [copies[chunk][(d + i) // 2, (d + i) % 2] for i in range(group)]
                    if group > 1:
                        got = [jnp.concatenate([g.astype(jnp.float32) for g in got], axis=0).astype(jnp.bfloat16)]
                    c_up[d * rows : (d + group) * rows, first : first + wide] = got[0]
                return
            for j in range(wide // LANES):
                value = copies[chunk][:, :, :, j * LANES : (j + 1) * LANES].astype(jnp.float32)
                value = turn(value.reshape(n * rows, LANES)).astype(jnp.bfloat16)
                low = first + j * LANES
                if kind == "down":
                    c_down[low : low + LANES, :] = value
                    continue
                for k, out in enumerate((c_query, c_key) if kind == "qk" else (c_value, c_mixed)):
                    top, bottom = max(low, k * heads), min(low + LANES, (k + 1) * heads)
                    if top < bottom:
                        out[top - k * heads : bottom - k * heads, :] = value[top - low : bottom - low]

        bodies = [prep, start_y, step_z, half_z, finish, start_pair, hop, end]
        first_finish = [e[0] for e in order].index(FINISH)
        marks = {first_finish: [smalls]}
        for place, body in ((1, norm_update), (2, norm_end)):
            marks.setdefault(first_finish + place * (len(order) - first_finish) // 3, []).append(body)
        barrier_done, late = False, []
        left = {kind: [c[0] for c in chunks].count(kind) for kind in ("up", "down", "vm", "qk")}
        for k, (kind, chunk, arg) in enumerate(order):
            if kind != PREP and not barrier_done:
                pl.semaphore_wait(barrier, n - 1)
                barrier_done = True
                late_norm = True
            for body in marks.get(k, []):
                body()
            bodies[kind](chunk, arg)
            if kind == FINISH:
                left[chunks[chunk][0]] -= 1
                if chunks[chunk][0] in pair and left[chunks[chunk][0]] == 0:
                    pairs_end(chunks[chunk][0])
            if kind == START + 0 or kind == STEP:
                if barrier_done and late_norm:
                    norm_start()
                    late_norm = False
            if kind == END:
                late.append(chunk)
                if len(late) > 2:
                    drain(late.pop(0))
        for chunk in late:
            drain(chunk)

    if orders:
        place = jnp.minimum(z, L - 1 - z)
        mirror = (2 * z) // L
        for zm, order in enumerate(orders):
            pl.when(place == zm)(functools.partial(program, order, zm, mirror))
    else:
        program(plain_order(L, chunks), z, 0)


def hand_on(count, *refs):
    given, out, sem = refs[:count], refs[count : 2 * count], refs[2 * count]
    writes = [pltpu.make_async_copy(given[i], out[i], sem.at[i]) for i in range(count)]
    for write in writes:
        write.start()
    for write in writes:
        write.wait()


def solution(mesh):
    n = mesh.shape["data"]
    L = n // 2

    def on_device(*args):
        grads, weights, moments = args[:7], args[7:14], args[14:]
        rows = weights[0].shape[0]
        cols = grads[0].shape[2]
        grads = [g[0].T if i in (2, 3, 4) else g[0] for i, g in enumerate(grads[:6])] + [grads[6]]
        grads[0] = grads[0].reshape(n, rows, cols)
        heads = grads[2].shape[0]
        weights = list(weights[:6]) + [weights[6].reshape(1, rows)]
        moments = list(moments[:6]) + [moments[6].reshape(1, rows)]
        weights[1], moments[1] = weights[1].T, moments[1].T
        chunks = make_chunks(cols, heads, PLAN)
        orders = ORDERS if len(ORDERS) == L // 2 and len(chunks) == len(PLAN) else None
        count = len(chunks)
        wide_norm = round_up(rows, LANES)
        copy_shapes = [(n * rows, cols), grads[1].shape] + [g.shape for g in grads[2:6]]
        out_shape = (
            [pltpu.VMEM(s, jnp.bfloat16) for s in copy_shapes]
            + [pltpu.VMEM((1, n * rows), jnp.float32)]
            + [pltpu.VMEM(w.shape, jnp.float32) for w in weights] * 2
        )
        scratch = [pltpu.VMEM(w.shape, jnp.float32) for w in weights + moments]
        scratch += [pltpu.VMEM((rows, 2 * heads), jnp.float32)] * 8
        bf16 = jnp.bfloat16
        scratch += [pltpu.VMEM((c[2], n * rows) if c[0] != "up" else (SUB, LANES), jnp.float32) for c in chunks]
        scratch += [pltpu.VMEM((n, rows, c[2]), jnp.float32) for c in chunks]
        for tall, dtype in ((rows, bf16), (1, jnp.float32)):
            for _ in range(2):
                scratch += [pltpu.VMEM((L if c[3] else 1, tall, c[2]), dtype) for c in chunks]
            for slots in (L, L + 1):
                scratch += [pltpu.VMEM((slots, 1 if c[3] else 2, tall, c[2]), dtype) for c in chunks]
        scratch += [pltpu.VMEM((L, 2, rows, c[2]), bf16) for c in chunks]
        scratch += [
            pltpu.VMEM((1, n * rows), jnp.float32),
            pltpu.VMEM((n, 1, n * rows), jnp.float32),
            pltpu.VMEM((n, 1, wide_norm), jnp.float32),
        ]
        sem = pltpu.SemaphoreType.DMA
        scratch += [
            sem((2 * count + 15,)),
            sem((2, 2, count, L)),
            sem((2, 2, count, L + 1)),
            sem((2, count, L + 1)),
            sem((2, count, L)),
            sem((2, 2, n)),
        ]
        anywhere = pl.BlockSpec(memory_space=pl.ANY)
        hbm = pl.BlockSpec(memory_space=pltpu.HBM)
        vmem = pl.BlockSpec(memory_space=pltpu.VMEM)
        with jax.sharding.use_abstract_mesh(mesh.abstract_mesh):
            outs = pl.pallas_call(
                functools.partial(kernel, n, chunks, orders),
                out_shape=out_shape,
                in_specs=[hbm] * 21,
                out_specs=[vmem] * 21,
                scratch_shapes=scratch,
                compiler_params=pltpu.CompilerParams(
                    collective_id=0, has_side_effects=True, vmem_limit_bytes=48 * 2**20
                ),
            )(*[pltpu.with_memory_space_constraint(a, pltpu.HBM) for a in grads + weights + moments])
            total = len(outs)
            outs = pl.pallas_call(
                functools.partial(hand_on, total),
                out_shape=[jax.ShapeDtypeStruct(o.shape, o.dtype) for o in out_shape],
                in_specs=[vmem] * total,
                out_specs=[anywhere] * total,
                scratch_shapes=[sem((total,))],
                compiler_params=pltpu.CompilerParams(vmem_limit_bytes=2**20),
            )(*outs)
        outs = list(outs)
        for i in (2, 3, 4, 8, 15):
            outs[i] = outs[i].T
        outs[6] = outs[6].reshape(-1).astype(jnp.bfloat16)
        outs[13] = outs[13].reshape(-1)
        outs[20] = outs[20].reshape(-1)
        return tuple(outs)

    row, col, vec = P("data", "width"), P("width", "data"), P("data")
    part = (row, col, row, row, row, col, vec)
    return jax.shard_map(
        on_device,
        mesh=mesh,
        in_specs=(
            P("data", None, "width"),
            P("data", "width", None),
            P("data", None, "width"),
            P("data", None, "width"),
            P("data", None, "width"),
            P("data", "width", None),
            P("data", None),
        )
        + part
        + part,
        out_specs=(
            P(None, "width"),
            P("width", None),
            P(None, "width"),
            P(None, "width"),
            P(None, "width"),
            P("width", None),
            P(),
        )
        + part
        + part,
        check_vma=False,
    )
```

time: 117 us -> 80.3 us (0.69)
  Pallas kernels: 107 us -> 78.8 us
  local copies, waits for them, and re-layouts: 8.23 us -> 0 us
    pallas_call x1, Pallas kernels: 104 us -> 76.2 us  [on_device(): pl.pallas_call(functools.partial(kernel, n, chunks, orders), out_shape=ou...]
    unnamed x20 -> x0, local copies, waits for them, and re-layouts: 8.23 us -> none
where the time goes in v2:
time: 80.3 us; the launch traced here: 80.1 us
  Pallas kernels  78.8 us (98%)
    pallas_call x1, Pallas kernels, on_device(): pl.pallas_call(functools.partial(kernel, n, chunks, orders), out_shape=ou...  76.2 us
    pallas_call x1, Pallas kernels, on_device(): pl.pallas_call(functools.partial(hand_on, total), out_shape=[jax.ShapeDty...  2.63 us

profile of v2, /device:TPU:0, one launch (start us, length us, event | category | flops | bytes accessed | tf_op | source)
XLA Modules:
  0.0 80.1 jit_solution(17551644108392285660)
XLA Ops:
  0.7 76.2 %shard_map.364 = (bf16[768,768]{1,0:T(8,128)(2,1)S(1)}, bf16[768,768]{1,0:T(8,128)(2,1)S(1)}, bf16[192,768]{1,0:T(8,128)(2,1)S(1)}, bf16[192,768]{1,0:T(8,128)(2...) custom-call(f32[8,96,768]{2,1,0:T(8,128)} %bitcast.23, ...), custom_call_target="tpu_custom_call" | custom-call | tf_op jit(solution)/shard_map/pallas_call | solution.py:620
  76.9 2.6 %shard_map.365 = (bf16[768,768]{1,0:T(8,128)(2,1)}, bf16[768,768]{1,0:T(8,128)(2,1)}, bf16[192,768]{1,0:T(8,128)(2,1)}, bf16[192,768]{1,0:T(8,128)(2,1)}, bf16[1...) custom-call(bf16[768,768]{1,0:T(8,128)(2,1)S(1)} %get-tuple-element., ...), custom_call_target="tpu_custom_call" | custom-call | tf_op jit(solution)/shard_map/pallas_call | solution.py:631
  79.5 0.6 convert_reduce_fusion

commit v3 on v2

--- a/solution.py
+++ b/solution.py
@@ -11,6 +11,7 @@
 hold_rate = 0.9
 LANES = 128
 SUB = 8
+NORM = 6
 LOW, REACH = -125.0, 251.0
 TINY = 1e-30
 
@@ -28,36 +29,36 @@
 ]
 ORDERS = [
     [
-        (0, 0, 0), (2, 0, 0), (2, 0, 1), (0, 2, 0), (1, 2, 0), (1, 2, 2), (0, 4, 0), (0, 1, 0),
-        (2, 4, 0), (1, 1, 0), (0, 3, 0), (0, 5, 0), (2, 2, 0), (1, 2, 1), (1, 1, 1), (1, 3, 2),
-        (2, 1, 0), (1, 3, 1), (1, 3, 0), (1, 1, 3), (1, 1, 2), (1, 5, 0), (2, 0, 2), (1, 5, 2),
-        (2, 2, 1), (1, 5, 1), (1, 2, 3), (2, 4, 1), (2, 1, 1), (0, 8, 0), (0, 6, 0), (1, 8, 3),
-        (2, 3, 0), (2, 2, 2), (2, 3, 1), (1, 3, 3), (0, 7, 0), (2, 1, 2), (4, 1, 0), (3, 0, 0),
-        (1, 8, 2), (2, 3, 2), (2, 5, 0), (2, 5, 1), (1, 6, 1), (2, 4, 2), (2, 7, 0), (1, 6, 0),
-        (3, 4, 0), (4, 2, 0), (1, 8, 0), (4, 0, 0), (1, 6, 2), (2, 5, 2), (6, 2, -2), (6, 3, -1),
-        (2, 7, 1), (2, 6, 0), (1, 5, 3), (6, 1, -1), (1, 8, 1), (5, 0, 0), (2, 6, 1), (2, 7, 2),
-        (2, 8, 0), (6, 5, -1), (4, 4, 0), (4, 3, 0), (1, 6, 3), (5, 4, 0), (3, 7, 0), (6, 1, -3),
-        (2, 6, 2), (6, 2, -3), (4, 5, 0), (6, 0, -3), (2, 8, 1), (6, 2, -1), (6, 3, -2), (4, 6, 0),
-        (6, 0, -2), (4, 7, 0), (2, 8, 2), (6, 3, -3), (6, 5, -2), (4, 8, 0), (6, 6, -1), (6, 1, -2),
-        (5, 7, 0), (6, 7, -1), (6, 4, -1), (6, 6, -2), (6, 0, -1), (7, 3, 0), (6, 8, -1), (7, 1, 0),
-        (6, 5, -3), (7, 0, 0), (6, 4, -3), (7, 2, 0), (6, 6, -3), (6, 8, -2), (6, 8, -3), (7, 5, 0),
-        (6, 4, -2), (7, 6, 0), (7, 4, 0), (7, 8, 0), (6, 7, -2), (6, 7, -3), (7, 7, 0),
+        (0, 0, 0), (0, 1, 0), (2, 0, 0), (1, 1, 1), (1, 1, 0), (0, 2, 0), (0, 5, 0), (1, 1, 2),
+        (1, 5, 3), (1, 2, 1), (2, 0, 1), (0, 3, 0), (1, 3, 0), (2, 1, 1), (1, 2, 0), (1, 3, 1),
+        (0, 4, 0), (2, 1, 0), (2, 0, 2), (2, 4, 1), (2, 1, 2), (0, 8, 0), (1, 2, 2), (2, 2, 1),
+        (0, 6, 0), (1, 1, 3), (1, 5, 1), (1, 6, 0), (0, 7, 0), (1, 3, 2), (2, 3, 0), (2, 2, 0),
+        (2, 4, 0), (1, 5, 0), (2, 2, 2), (2, 7, 0), (1, 8, 2), (2, 6, 0), (3, 0, 0), (1, 6, 1),
+        (2, 3, 2), (2, 3, 1), (1, 8, 3), (1, 5, 2), (2, 5, 1), (1, 8, 0), (4, 0, 0), (1, 6, 2),
+        (2, 5, 0), (1, 6, 3), (2, 4, 2), (4, 1, 0), (1, 8, 1), (1, 2, 3), (1, 3, 3), (2, 5, 2),
+        (2, 7, 1), (5, 0, 0), (6, 1, -2), (2, 6, 1), (6, 3, -1), (6, 0, -1), (3, 4, 0), (4, 2, 0),
+        (2, 7, 2), (3, 7, 0), (2, 8, 0), (4, 4, 0), (6, 2, -1), (6, 1, -1), (2, 6, 2), (6, 3, -2),
+        (6, 2, -2), (4, 3, 0), (4, 7, 0), (2, 8, 1), (4, 5, 0), (4, 6, 0), (5, 4, 0), (2, 8, 2),
+        (6, 1, -3), (5, 7, 0), (6, 5, -1), (6, 0, -2), (4, 8, 0), (6, 4, -1), (6, 4, -2), (6, 2, -3),
+        (6, 5, -2), (6, 6, -2), (6, 6, -1), (6, 3, -3), (6, 0, -3), (6, 8, -1), (6, 8, -2), (6, 5, -3),
+        (7, 0, 0), (7, 2, 0), (7, 1, 0), (6, 4, -3), (7, 3, 0), (6, 6, -3), (6, 7, -1), (6, 8, -3),
+        (6, 7, -3), (7, 5, 0), (7, 6, 0), (7, 4, 0), (6, 7, -2), (7, 7, 0), (7, 8, 0),
     ],
     [
-        (0, 1, 0), (1, 1, 1), (0, 0, 0), (0, 3, 0), (1, 1, 3), (1, 1, 2), (0, 2, 0), (0, 5, 0),
-        (1, 2, 0), (1, 3, 0), (1, 2, 1), (1, 1, 0), (2, 0, 0), (0, 6, 0), (1, 2, 3), (2, 0, 1),
-        (0, 4, 0), (1, 3, 2), (2, 2, 0), (1, 2, 2), (2, 1, 0), (1, 3, 1), (2, 0, 2), (1, 5, 0),
-        (2, 4, 0), (1, 6, 2), (3, 0, 0), (2, 1, 2), (2, 2, 1), (1, 3, 3), (2, 2, 2), (0, 7, 0),
-        (2, 1, 1), (2, 4, 2), (2, 3, 0), (1, 5, 3), (1, 5, 2), (4, 2, 0), (2, 3, 1), (4, 0, 0),
-        (1, 5, 1), (2, 4, 1), (2, 3, 2), (6, 1, 1), (4, 1, 0), (6, 2, -1), (4, 3, 0), (2, 5, 0),
-        (5, 0, 0), (6, 1, -2), (0, 8, 0), (1, 6, 0), (3, 4, 0), (2, 5, 1), (6, 1, -1), (2, 5, 2),
-        (6, 0, -1), (6, 2, 1), (2, 7, 0), (4, 5, 0), (2, 7, 1), (4, 4, 0), (6, 3, -1), (1, 6, 1),
-        (6, 2, -2), (2, 7, 2), (1, 8, 0), (6, 0, 1), (2, 6, 0), (6, 5, -1), (2, 6, 1), (3, 7, 0),
-        (1, 6, 3), (5, 4, 0), (6, 0, -2), (2, 8, 0), (2, 6, 2), (6, 3, 1), (1, 8, 2), (6, 4, 1),
-        (6, 4, -1), (7, 0, 0), (1, 8, 1), (4, 7, 0), (4, 6, 0), (1, 8, 3), (6, 5, 1), (6, 3, -2),
-        (2, 8, 2), (6, 6, -1), (2, 8, 1), (6, 4, -2), (6, 6, 1), (5, 7, 0), (4, 8, 0), (6, 5, -2),
-        (7, 4, 0), (6, 6, -2), (6, 8, 1), (6, 8, -1), (6, 7, 1), (6, 8, -2), (6, 7, -1), (7, 2, 0),
-        (7, 3, 0), (6, 7, -2), (7, 7, 0), (7, 8, 0), (7, 1, 0), (7, 6, 0), (7, 5, 0),
+        (0, 1, 0), (1, 1, 1), (1, 1, 0), (0, 0, 0), (0, 3, 0), (0, 2, 0), (0, 5, 0), (1, 3, 0),
+        (0, 7, 0), (0, 8, 0), (1, 1, 3), (1, 1, 2), (1, 2, 0), (1, 5, 1), (2, 0, 0), (1, 3, 3),
+        (1, 3, 2), (0, 6, 0), (2, 0, 1), (2, 1, 1), (1, 2, 1), (0, 4, 0), (1, 3, 1), (2, 1, 0),
+        (3, 0, 0), (2, 4, 1), (1, 2, 3), (2, 0, 2), (1, 2, 2), (4, 1, 0), (2, 2, 1), (2, 3, 0),
+        (4, 0, 0), (2, 2, 0), (2, 1, 2), (1, 6, 1), (6, 1, -1), (2, 4, 0), (1, 6, 0), (1, 5, 0),
+        (1, 6, 2), (4, 2, 0), (5, 0, 0), (2, 3, 2), (2, 4, 2), (2, 7, 0), (1, 6, 3), (1, 5, 3),
+        (2, 2, 2), (2, 3, 1), (1, 5, 2), (6, 0, -1), (6, 2, -1), (2, 6, 0), (2, 5, 1), (2, 5, 0),
+        (4, 3, 0), (2, 6, 2), (3, 4, 0), (6, 1, 1), (2, 7, 2), (4, 5, 0), (2, 7, 1), (4, 4, 0),
+        (1, 8, 2), (6, 3, -1), (1, 8, 0), (1, 8, 1), (6, 1, -2), (6, 0, 1), (2, 5, 2), (2, 6, 1),
+        (5, 4, 0), (6, 5, -1), (6, 2, 1), (6, 0, -2), (2, 8, 0), (3, 7, 0), (1, 8, 3), (4, 6, 0),
+        (6, 4, -1), (6, 3, 1), (2, 8, 2), (2, 8, 1), (6, 5, 1), (6, 2, -2), (6, 6, 1), (7, 1, 0),
+        (4, 7, 0), (6, 6, -1), (6, 3, -2), (6, 4, 1), (4, 8, 0), (6, 5, -2), (6, 6, -2), (6, 7, 1),
+        (6, 4, -2), (6, 8, -1), (6, 8, 1), (5, 7, 0), (6, 8, -2), (6, 7, -2), (6, 7, -1), (7, 7, 0),
+        (7, 2, 0), (7, 4, 0), (7, 0, 0), (7, 8, 0), (7, 5, 0), (7, 6, 0), (7, 3, 0),
     ],
 ]
 
@@ -243,10 +244,6 @@
     start(small[1:])
 
     barrier = pltpu.get_barrier_semaphore()
-    for step in range(1, n):
-        pl.semaphore_signal(
-            barrier, inc=1, device_id={"data": (me + step) % n}, device_id_type=pl.DeviceIdType.MESH
-        )
 
     def norm_copies(give):
         src, dst = (g_norm, norm_hold) if give else (norm_copy.at[me], norm_copy)
@@ -516,6 +513,14 @@
                     if top < bottom:
                         out[top - k * heads : bottom - k * heads, :] = value[top - low : bottom - low]
 
+        def greet(there):
+            pl.semaphore_signal(
+                barrier, inc=1, device_id={"data": there}, device_id_type=pl.DeviceIdType.MESH
+            )
+
+        greet(partner)
+        when(has_near, lambda: greet(2 * real(zm - 1) + y))
+        when(has_far, lambda: greet(2 * real(zm + 1) + y))
         bodies = [prep, start_y, step_z, half_z, finish, start_pair, hop, end]
         first_finish = [e[0] for e in order].index(FINISH)
         marks = {first_finish: [smalls]}
@@ -525,20 +530,17 @@
         left = {kind: [c[0] for c in chunks].count(kind) for kind in ("up", "down", "vm", "qk")}
         for k, (kind, chunk, arg) in enumerate(order):
             if kind != PREP and not barrier_done:
-                pl.semaphore_wait(barrier, n - 1)
+                pl.semaphore_wait(barrier, 1 + pick(has_near, 1, 0) + pick(has_far, 1, 0))
                 barrier_done = True
-                late_norm = True
             for body in marks.get(k, []):
                 body()
             bodies[kind](chunk, arg)
+            if k == first_finish:
+                norm_start()
             if kind == FINISH:
                 left[chunks[chunk][0]] -= 1
                 if chunks[chunk][0] in pair and left[chunks[chunk][0]] == 0:
                     pairs_end(chunks[chunk][0])
-            if kind == START + 0 or kind == STEP:
-                if barrier_done and late_norm:
-                    norm_start()
-                    late_norm = False
             if kind == END:
                 late.append(chunk)
                 if len(late) > 2:
@@ -557,9 +559,10 @@
 
 def hand_on(count, *refs):
     given, out, sem = refs[:count], refs[count : 2 * count], refs[2 * count]
-    writes = [pltpu.make_async_copy(given[i], out[i], sem.at[i]) for i in range(count)]
+    writes = [pltpu.make_async_copy(given[i], out[i], sem.at[i]) for i in range(count) if i != NORM]
     for write in writes:
         write.start()
+    out[NORM][...] = given[NORM][...].reshape(-1).astype(jnp.bfloat16)
     for write in writes:
         write.wait()
 
@@ -630,16 +633,18 @@
             total = len(outs)
             outs = pl.pallas_call(
                 functools.partial(hand_on, total),
-                out_shape=[jax.ShapeDtypeStruct(o.shape, o.dtype) for o in out_shape],
+                out_shape=[
+                    jax.ShapeDtypeStruct((o.size,), bf16) if i == NORM else jax.ShapeDtypeStruct(o.shape, o.dtype)
+                    for i, o in enumerate(outs)
+                ],
                 in_specs=[vmem] * total,
-                out_specs=[anywhere] * total,
+                out_specs=[vmem if i == NORM else anywhere for i in range(total)],
                 scratch_shapes=[sem((total,))],
                 compiler_params=pltpu.CompilerParams(vmem_limit_bytes=2**20),
             )(*outs)
         outs = list(outs)
         for i in (2, 3, 4, 8, 15):
             outs[i] = outs[i].T
-        outs[6] = outs[6].reshape(-1).astype(jnp.bfloat16)
         outs[13] = outs[13].reshape(-1)
         outs[20] = outs[20].reshape(-1)
         return tuple(outs)

time: 80.3 us -> 77.6 us (0.966)
  Pallas kernels: 78.8 us -> 76.6 us
    pallas_call x1, Pallas kernels: 76.2 us -> 73.4 us  [on_device(): pl.pallas_call(functools.partial(kernel, n, chunks, orders), out_shape=ou...]
where the time goes in v3:
time: 77.6 us; the launch traced here: 77.4 us
  Pallas kernels  76.6 us (99%)
  between operations  0.84 us (1%)
    pallas_call x1, Pallas kernels, on_device(): pl.pallas_call(functools.partial(kernel, n, chunks, orders), out_shape=ou...  73.4 us
    pallas_call x1, Pallas kernels, on_device(): pl.pallas_call(functools.partial(hand_on, total), out_shape=[jax.ShapeDty...  3.2 us

profile of v3, /device:TPU:0, one launch (start us, length us, event | category | flops | bytes accessed | tf_op | source)
XLA Modules:
  0.0 77.4 jit_solution(399932667033550369)
XLA Ops:
  0.7 73.4 %shard_map.364 = (bf16[768,768]{1,0:T(8,128)(2,1)S(1)}, bf16[768,768]{1,0:T(8,128)(2,1)S(1)}, bf16[192,768]{1,0:T(8,128)(2,1)S(1)}, bf16[192,768]{1,0:T(8,128)(2...) custom-call(f32[8,96,768]{2,1,0:T(8,128)} %bitcast.23, ...), custom_call_target="tpu_custom_call" | custom-call | tf_op jit(solution)/shard_map/pallas_call | solution.py:623
  74.0 3.2 %shard_map.365 = (bf16[768,768]{1,0:T(8,128)(2,1)}, bf16[768,768]{1,0:T(8,128)(2,1)}, bf16[192,768]{1,0:T(8,128)(2,1)}, bf16[192,768]{1,0:T(8,128)(2,1)}, bf16[1...) custom-call(bf16[768,768]{1,0:T(8,128)(2,1)S(1)} %get-tuple-element., ...), custom_call_target="tpu_custom_call" | custom-call | tf_op jit(solution)/shard_map/pallas_call | solution.py:634
